TPU v7x, 32 devices: a whole 2x2x4 slice. The times are simulated.
32 devices in a mesh: mp: 8 (over z, y), dp: 4 (over x, core).
Axes of the slice: x: 2, y: 2, z: 4, core: 2. Of those that a mesh axis runs over, the one named last changes fastest.
Arguments:
- features: bfloat16 [32, 4, 4, 512], P(('dp', 'mp')), may hold values from 0 to 2
- labels: int32 [32], P('dp'), may hold values from 0 to 9
- subset_ids: int32 [8], P('mp'), may hold values from 0 to 255
- conv1_weight: bfloat16 [8, 9, 512, 512], P('mp'), may hold values from -0.09375 to 0.09375
- conv2_weight: bfloat16 [8, 9, 512, 512], P('mp'), may hold values from -0.09375 to 0.09375
- head_weight: float32 [8, 512, 10], P('mp'), may hold values from -0.25 to 0.25
Outputs:
- datamodel: float32 [32, 256], P(('dp', 'mp'))
- margin_mean: float32 [32], P(('dp', 'mp'))
- margin_norm: float32 [32], P(('dp', 'mp'))
All inputs are finite; a program needn't handle non-finite values.
Results may differ from a plain program's by a relative error of at most 0.00077.
Values may be sent and summed in bfloat16 or wider, within the bound.
A program may use at most 128 MiB of HBM per device.

v0:
```python
import jax
import jax.numpy as jnp
from jax import lax
from jax.sharding import PartitionSpec as P

SUBSETS = 256


def convolve(grid, kernel):
    batch = grid.shape[0]
    width = grid.shape[1]
    chans = grid.shape[3]
    padded = jnp.pad(grid, ((0, 0), (1, 1), (1, 1), (0, 0)))
    result = jnp.zeros((batch * width * width, kernel.shape[2]), jnp.float32)
    for offset in range(9):
        row_off, col_off = divmod(offset, 3)
        shifted = padded[:, row_off : row_off + width, col_off : col_off + width, :].reshape(
            batch * width * width, chans
        )
        result = result + jnp.dot(shifted, kernel[offset], preferred_element_type=jnp.float32)
    return result


def margins_of(grid, first_kernel, second_kernel, head, target_labels):
    batch = grid.shape[0]
    width = grid.shape[1]
    chans = grid.shape[3]
    hidden = (
        jax.nn.relu(convolve(grid, first_kernel))
        .astype(jnp.bfloat16)
        .reshape(batch, width, width, chans)
    )
    branch = jax.nn.relu(convolve(hidden, second_kernel))
    blocked = grid.astype(jnp.float32).reshape(batch * width * width, chans) + branch
    pooled = jnp.max(blocked.reshape(batch, width * width, chans), axis=1)
    logits = jnp.dot(
        pooled, head, precision=lax.Precision.HIGHEST, preferred_element_type=jnp.float32
    )
    classes = jnp.arange(head.shape[1], dtype=jnp.int32)[None, :]
    chosen = classes == target_labels[:, None]
    correct = jnp.sum(jnp.where(chosen, logits, 0.0), axis=1)
    rival = jnp.max(jnp.where(chosen, -1e30, logits), axis=1)
    return correct - rival


def subset_table(identity):
    return (identity[:, None] == jnp.arange(SUBSETS, dtype=jnp.int32)[None, :]).astype(jnp.float32)


def shards(features, labels, subset_ids, conv1_weight, conv2_weight, head_weight):
    models_dev = conv1_weight.shape[0]
    model_count = models_dev * lax.axis_size("mp")
    rows_out = [
        margins_of(
            lax.all_gather(features, "mp", axis=0, tiled=True),
            conv1_weight[0],
            conv2_weight[0],
            head_weight[0],
            labels,
        )
    ]
    margin = jnp.stack(rows_out, 0)
    columns = lax.all_to_all(margin, "mp", split_axis=1, concat_axis=0, tiled=True)
    every_id = lax.all_gather(subset_ids, "mp", axis=0, tiled=True)
    margin_mean = jnp.sum(columns, axis=0) / model_count
    centred = columns - margin_mean[None, :]
    margin_norm = jnp.sqrt(1.0 + jnp.sum(centred * centred, axis=0) / model_count)
    scaled = centred / margin_norm[None, :]
    datamodel = jnp.dot(
        scaled.T,
        subset_table(every_id),
        precision=lax.Precision.HIGHEST,
        preferred_element_type=jnp.float32,
    )
    return (datamodel, margin_mean, margin_norm)


def solution(mesh):
    in_specs = (
        P(("dp", "mp"), None, None, None),
        P("dp"),
        P("mp"),
        P("mp", None, None, None),
        P("mp", None, None, None),
        P("mp", None, None),
    )
    out_specs = (P(("dp", "mp"), None), P(("dp", "mp")), P(("dp", "mp")))
    return jax.shard_map(shards, mesh=mesh, in_specs=in_specs, out_specs=out_specs, check_vma=False)
```

profile of v0, /device:TPU:0, one launch (start us, length us, event | category | flops | bytes accessed | tf_op | source)
XLA Modules:
  0.0 84.1 jit_solution(346595920201907699)
XLA Ops:
  0.6 32.5 %all_gather.6 = bf16[8,4,4,512]{3,2,1,0:T(4,128)(2,1)S(1)} all-gather(bf16[1,4,4,512]{3,2,1,0:T(4,128)(2,1)} %param.6), channel_id=1, replica_groups=mesh['mp'=8,'dp'=4] {'mp'}, dimensions={0}, use_global_device_ids=true | all-gather | bytes 147456 | tf_op jit(solution)/shard_map/all_gather | solution.py:55
  34.0 1.3 %fusion.22 = f32[128,512]{1,0:T(8,128)S(1)} fusion(bf16[128,512]{1,0:T(8,128)(2,1)S(1)} %reshape.174, bf16[1,9,512,512]{3,2,1,0:T(8,128)(2,1)} %param.9), kind=kOutput, calls=%fused_computation.54 | convolution fusion | flops 67108864 | bytes 917504 | tf_op jit(solution)/shard_map/dot_general | solution.py:20
  35.3 1.3 %convolution_add_fusion.15 = f32[128,512]{1,0:T(8,128)S(1)} fusion(f32[128,512]{1,0:T(8,128)S(1)} %fusion.22, bf16[128,512]{1,0:T(8,128)(2,1)S(1)} %reshape.175, bf16[1,9,512,512]{3,2,1,0:T(8,128)(2,1)} %param.9), kind=kOutput, calls=%fused_computation.15 | convolution fusion | flops 67174400 | bytes 1179648 | tf_op jit(solution)/shard_map/dot_general | solution.py:20
  36.6 1.3 %convolution_add_fusion.14 = f32[128,512]{1,0:T(8,128)S(1)} fusion(f32[128,512]{1,0:T(8,128)S(1)} %convolution_add_fusion.15, bf16[128,512]{1,0:T(8,128)(2,1)S(1)} %reshape.176, bf16[1,9,512,512]{3,2,1,0:T(8,128)(2,1)} %param.9), kind=kOutput, calls=%fused_computation.14 | convolution fusion | flops 67174400 | bytes 1179648 | tf_op jit(solution)/shard_map/dot_general | solution.py:20
  37.9 1.3 %convolution_add_fusion.13 = f32[128,512]{1,0:T(8,128)S(1)} fusion(f32[128,512]{1,0:T(8,128)S(1)} %convolution_add_fusion.14, bf16[128,512]{1,0:T(8,128)(2,1)S(1)} %reshape.177, bf16[1,9,512,512]{3,2,1,0:T(8,128)(2,1)} %param.9), kind=kOutput, calls=%fused_computation.13 | convolution fusion | flops 67174400 | bytes 1179648 | tf_op jit(solution)/shard_map/dot_general | solution.py:20
  39.1 1.3 %convolution_add_fusion.12 = f32[128,512]{1,0:T(8,128)S(1)} fusion(f32[128,512]{1,0:T(8,128)S(1)} %convolution_add_fusion.13, bf16[128,512]{1,0:T(8,128)(2,1)S(1)} %reshape.172, bf16[1,9,512,512]{3,2,1,0:T(8,128)(2,1)} %param.9), kind=kOutput, calls=%fused_computation.12 | convolution fusion | flops 67174400 | bytes 1179648 | tf_op jit(solution)/shard_map/dot_general | solution.py:20
  40.4 1.3 %convolution_add_fusion.11 = f32[128,512]{1,0:T(8,128)S(1)} fusion(f32[128,512]{1,0:T(8,128)S(1)} %convolution_add_fusion.12, bf16[128,512]{1,0:T(8,128)(2,1)S(1)} %reshape.178, bf16[1,9,512,512]{3,2,1,0:T(8,128)(2,1)} %param.9), kind=kOutput, calls=%fused_computation.11 | convolution fusion | flops 67174400 | bytes 1179648 | tf_op jit(solution)/shard_map/dot_general | solution.py:20
  41.7 1.3 %convolution_add_fusion.10 = f32[128,512]{1,0:T(8,128)S(1)} fusion(f32[128,512]{1,0:T(8,128)S(1)} %convolution_add_fusion.11, bf16[128,512]{1,0:T(8,128)(2,1)S(1)} %reshape.179, bf16[1,9,512,512]{3,2,1,0:T(8,128)(2,1)} %param.9), kind=kOutput, calls=%fused_computation.10 | convolution fusion | flops 67174400 | bytes 1179648 | tf_op jit(solution)/shard_map/dot_general | solution.py:20
  43.0 1.3 %convolution_add_fusion.9 = f32[128,512]{1,0:T(8,128)S(1)} fusion(f32[128,512]{1,0:T(8,128)S(1)} %convolution_add_fusion.10, bf16[128,512]{1,0:T(8,128)(2,1)S(1)} %reshape.180, bf16[1,9,512,512]{3,2,1,0:T(8,128)(2,1)} %param.9), kind=kOutput, calls=%fused_computation.9 | convolution fusion | flops 67174400 | bytes 1179648 | tf_op jit(solution)/shard_map/dot_general | solution.py:20
  44.3 1.3 %fusion.3 = bf16[128,512]{1,0:T(8,128)(2,1)S(1)} fusion(f32[128,512]{1,0:T(8,128)S(1)} %convolution_add_fusion.9, bf16[128,512]{1,0:T(8,128)(2,1)S(1)} %reshape.181, bf16[1,9,512,512]{3,2,1,0:T(8,128)(2,1)} %param.9), kind=kOutput, calls=%fused_computation.19 | convolution fusion | flops 67305472 | bytes 1048576 | tf_op jit(solution)/shard_map/dot_general | solution.py:20
  46.2 1.3 %fusion.12 = f32[128,512]{1,0:T(8,128)S(1)} fusion(bf16[128,512]{1,0:T(8,128)(2,1)S(1)} %reshape.183, bf16[1,9,512,512]{3,2,1,0:T(8,128)(2,1)} %param.10), kind=kOutput, calls=%fused_computation.44 | convolution fusion | flops 67108864 | bytes 917504 | tf_op jit(solution)/shard_map/dot_general | solution.py:20
  47.5 1.3 %convolution_add_fusion.7 = f32[128,512]{1,0:T(8,128)S(1)} fusion(f32[128,512]{1,0:T(8,128)S(1)} %fusion.12, bf16[128,512]{1,0:T(8,128)(2,1)S(1)} %reshape.184, bf16[1,9,512,512]{3,2,1,0:T(8,128)(2,1)} %param.10), kind=kOutput, calls=%fused_computation.7 | convolution fusion | flops 67174400 | bytes 1179648 | tf_op jit(solution)/shard_map/dot_general | solution.py:20
  48.8 1.3 %convolution_add_fusion.6 = f32[128,512]{1,0:T(8,128)S(1)} fusion(f32[128,512]{1,0:T(8,128)S(1)} %convolution_add_fusion.7, bf16[128,512]{1,0:T(8,128)(2,1)S(1)} %reshape.185, bf16[1,9,512,512]{3,2,1,0:T(8,128)(2,1)} %param.10), kind=kOutput, calls=%fused_computation.6 | convolution fusion | flops 67174400 | bytes 1179648 | tf_op jit(solution)/shard_map/dot_general | solution.py:20
  50.1 1.3 %convolution_add_fusion.5 = f32[128,512]{1,0:T(8,128)S(1)} fusion(f32[128,512]{1,0:T(8,128)S(1)} %convolution_add_fusion.6, bf16[128,512]{1,0:T(8,128)(2,1)S(1)} %reshape.186, bf16[1,9,512,512]{3,2,1,0:T(8,128)(2,1)} %param.10), kind=kOutput, calls=%fused_computation.5 | convolution fusion | flops 67174400 | bytes 1179648 | tf_op jit(solution)/shard_map/dot_general | solution.py:20
  51.4 1.3 %convolution_add_fusion.4 = f32[128,512]{1,0:T(8,128)S(1)} fusion(f32[128,512]{1,0:T(8,128)S(1)} %convolution_add_fusion.5, bf16[128,512]{1,0:T(8,128)(2,1)S(1)} %fusion.3, bf16[1,9,512,512]{3,2,1,0:T(8,128)(2,1)} %param.10), kind=kOutput, calls=%fused_computation.4 | convolution fusion | flops 67174400 | bytes 1179648 | tf_op jit(solution)/shard_map/dot_general | solution.py:20
  52.8 1.3 %convolution_add_fusion.3 = f32[128,512]{1,0:T(8,128)S(1)} fusion(f32[128,512]{1,0:T(8,128)S(1)} %convolution_add_fusion.4, bf16[128,512]{1,0:T(8,128)(2,1)S(1)} %reshape.187, bf16[1,9,512,512]{3,2,1,0:T(8,128)(2,1)} %param.10), kind=kOutput, calls=%fused_computation.3 | convolution fusion | flops 67174400 | bytes 1179648 | tf_op jit(solution)/shard_map/dot_general | solution.py:20
  54.1 1.3 %convolution_add_fusion.2 = f32[128,512]{1,0:T(8,128)S(1)} fusion(f32[128,512]{1,0:T(8,128)S(1)} %convolution_add_fusion.3, bf16[128,512]{1,0:T(8,128)(2,1)S(1)} %reshape.188, bf16[1,9,512,512]{3,2,1,0:T(8,128)(2,1)} %param.10), kind=kOutput, calls=%fused_computation.2 | convolution fusion | flops 67174400 | bytes 1179648 | tf_op jit(solution)/shard_map/dot_general | solution.py:20
  55.4 1.3 %convolution_add_fusion.1 = f32[128,512]{1,0:T(8,128)S(1)} fusion(f32[128,512]{1,0:T(8,128)S(1)} %convolution_add_fusion.2, bf16[128,512]{1,0:T(8,128)(2,1)S(1)} %reshape.189, bf16[1,9,512,512]{3,2,1,0:T(8,128)(2,1)} %param.10), kind=kOutput, calls=%fused_computation.1 | convolution fusion | flops 67174400 | bytes 1179648 | tf_op jit(solution)/shard_map/dot_general | solution.py:20
  56.7 1.3 %bitcast_reduce_fusion = f32[8,512]{1,0:T(8,128)S(1)} fusion(f32[128,512]{1,0:T(8,128)S(1)} %convolution_add_fusion.1, bf16[128,512]{1,0:T(8,128)(2,1)S(1)} %reshape.190, bf16[1,9,512,512]{3,2,1,0:T(8,128)(2,1)} %param.10, bf16[128,512]{1,0:T(8,128)(2,1)S(1)} %reshape.172), kind=kOutput, calls=%fused_computation.74 | convolution fusion | flops 67432448 | bytes 1064960 | tf_op jit(solution)/shard_map/dot_general | solution.py:20
  58.3 0.7 copy.10
  60.2 0.8 dynamic-update-slice
  61.0 5.5 %all-to-all-start = ((f32[1,8,1]{2,0,1:T(1,128)}), f32[1,8,1]{2,0,1:T(1,128)S(1)}, u32[]{:S(2)}, u32[]{:S(2)}) async-start(f32[1,8,1]{2,0,1:T(1,128)} %copy.10), calls=%async_computation | async-start | bytes 8192 | tf_op jit(solution)/shard_map/all_to_all | solution.py:63
  66.5 11.9 %all-reduce.2 = s32[8]{0:T(128)S(1)} all-reduce(s32[8]{0:T(128)S(1)} %dynamic-update-slice), channel_id=1, replica_groups=mesh['mp'=8,'dp'=4] {'mp'}, use_global_device_ids=true, to_apply=%add.2 | all-reduce | flops 8 | bytes 64
  81.1 0.8 fusion.47
  (34 shorter events, 3.9 us)
Async XLA Ops:
  48.8 9.2 %copy-start = (f32[1,512,10]{1,0,2:T(1,128)S(1)}, f32[1,512,10]{1,0,2:T(1,128)}, u32[]{:S(2)}) copy-start(f32[1,512,10]{1,0,2:T(1,128)} %param.11) | copy-start | bytes 61444
  48.8 9.2 %copy-start.1 = (s32[8]{0:T(128)S(1)}, s32[8]{0:T(128)}, u32[]{:S(2)}) copy-start(s32[8]{0:T(128)} %param.7) | copy-start | bytes 100
  48.8 10.8 %copy-start.2 = (u32[32]{0:T(128)S(1)}, u32[32]{0:T(128)}, u32[]{:S(2)}) copy-start(u32[32]{0:T(128)} %constant.32) | copy-start | bytes 388
  61.0 17.4 %all-to-all-start = ((f32[1,8,1]{2,0,1:T(1,128)}), f32[1,8,1]{2,0,1:T(1,128)S(1)}, u32[]{:S(2)}, u32[]{:S(2)}) async-start(f32[1,8,1]{2,0,1:T(1,128)} %copy.10), calls=%async_computation | async-start | bytes 8192 | tf_op jit(solution)/shard_map/all_to_all | solution.py:63
where the time goes:
time: 85.2 us; the launch traced here: 84.1 us
  blocking collectives  44.4 us (52%)
  matrix products  24 us (28%)
  starting transfers between devices  5.52 us (6%)
  between operations  5.14 us (6%)
  local copies, waits for them, and re-layouts  3.67 us (4%)
  other arithmetic  1.37 us (2%)
    all_gather x1, blocking collectives, shards(): lax.all_gather(features, 'mp', axis=0, tiled=True)  32.5 us
    dot_general x18, matrix products, convolve(): jnp.dot(shifted, kernel[offset], preferred_element_type=jnp.float32)  23 us
    unnamed x1, blocking collectives  11.9 us
    all_to_all x1, starting transfers between devices, shards(): lax.all_to_all(margin, 'mp', split_axis=1, concat_axis=0, tiled=True)  5.52 us
  transfers between devices with their start and end apart: 1, of which 0 were waited for; matrix products, arithmetic and copies ran while one was open for 0% of the time, Pallas kernels for 0%

commit v1 on v0

--- a/solution.py
+++ b/solution.py
@@ -60,7 +60,14 @@
         )
     ]
     margin = jnp.stack(rows_out, 0)
-    columns = lax.all_to_all(margin, "mp", split_axis=1, concat_axis=0, tiled=True)
+
+    def prepare_entries(in_array, on_dim, which_dim=0):
+        return jnp.concatenate(
+            lax.all_to_all(jnp.stack(jnp.split(in_array, lax.psum(1, "mp"), on_dim)), "mp", 0, 0),
+            axis=which_dim,
+        )
+
+    columns = prepare_entries(margin, 1)
     every_id = lax.all_gather(subset_ids, "mp", axis=0, tiled=True)
     margin_mean = jnp.sum(columns, axis=0) / model_count
     centred = columns - margin_mean[None, :]

time: 85.2 us -> 94.6 us (1.11)
  local copies, waits for them, and re-layouts: 3.67 us -> 13 us
    unnamed x9 -> x16, local copies, waits for them, and re-layouts: 1.36 us -> 9.54 us
    another operation x0 -> x1, local copies, waits for them, and re-layouts: none -> 1.17 us  [prepare_entries(): jnp.stack(jnp.split(in_array, lax.psum(1, 'mp'), on_dim))]
where the time goes in v1:
time: 94.6 us; the launch traced here: 93.4 us
  blocking collectives  44.4 us (47%)
  matrix products  24 us (25%)
  local copies, waits for them, and re-layouts  13 us (14%)
  starting transfers between devices  5.52 us (6%)
  between operations  5.13 us (5%)
  other arithmetic  1.37 us (1%)
    all_gather x1, blocking collectives, shards(): lax.all_gather(features, 'mp', axis=0, tiled=True)  32.5 us
    dot_general x18, matrix products, convolve(): jnp.dot(shifted, kernel[offset], preferred_element_type=jnp.float32)  23 us
    unnamed x1, blocking collectives  11.9 us
    unnamed x16, local copies, waits for them, and re-layouts  9.54 us
    all_to_all x1, starting transfers between devices, prepare_entries(): lax.all_to_all(jnp.stack(jnp.split(in_array, lax.psum(1, 'mp'), on_dim)),...  5.52 us
  transfers between devices with their start and end apart: 1, of which 0 were waited for; matrix products, arithmetic and copies ran while one was open for 0% of the time, Pallas kernels for 0%

profile of v1, /device:TPU:0, one launch (start us, length us, event | category | flops | bytes accessed | tf_op | source)
XLA Modules:
  0.0 93.4 jit_solution(11981454319280243044)
XLA Ops:
  0.6 32.5 %all_gather.6 = bf16[8,4,4,512]{3,2,1,0:T(4,128)(2,1)S(1)} all-gather(bf16[1,4,4,512]{3,2,1,0:T(4,128)(2,1)} %param.6), channel_id=1, replica_groups=mesh['mp'=8,'dp'=4] {'mp'}, dimensions={0}, use_global_device_ids=true | all-gather | bytes 147456 | tf_op jit(solution)/shard_map/all_gather | solution.py:55
  34.0 1.3 %fusion.22 = f32[128,512]{1,0:T(8,128)S(1)} fusion(bf16[128,512]{1,0:T(8,128)(2,1)S(1)} %reshape.168, bf16[1,9,512,512]{3,2,1,0:T(8,128)(2,1)} %param.9), kind=kOutput, calls=%fused_computation.54 | convolution fusion | flops 67108864 | bytes 917504 | tf_op jit(solution)/shard_map/dot_general | solution.py:20
  35.3 1.3 %convolution_add_fusion.15 = f32[128,512]{1,0:T(8,128)S(1)} fusion(f32[128,512]{1,0:T(8,128)S(1)} %fusion.22, bf16[128,512]{1,0:T(8,128)(2,1)S(1)} %reshape.169, bf16[1,9,512,512]{3,2,1,0:T(8,128)(2,1)} %param.9), kind=kOutput, calls=%fused_computation.15 | convolution fusion | flops 67174400 | bytes 1179648 | tf_op jit(solution)/shard_map/dot_general | solution.py:20
  36.6 1.3 %convolution_add_fusion.14 = f32[128,512]{1,0:T(8,128)S(1)} fusion(f32[128,512]{1,0:T(8,128)S(1)} %convolution_add_fusion.15, bf16[128,512]{1,0:T(8,128)(2,1)S(1)} %reshape.170, bf16[1,9,512,512]{3,2,1,0:T(8,128)(2,1)} %param.9), kind=kOutput, calls=%fused_computation.14 | convolution fusion | flops 67174400 | bytes 1179648 | tf_op jit(solution)/shard_map/dot_general | solution.py:20
  37.9 1.3 %convolution_add_fusion.13 = f32[128,512]{1,0:T(8,128)S(1)} fusion(f32[128,512]{1,0:T(8,128)S(1)} %convolution_add_fusion.14, bf16[128,512]{1,0:T(8,128)(2,1)S(1)} %reshape.171, bf16[1,9,512,512]{3,2,1,0:T(8,128)(2,1)} %param.9), kind=kOutput, calls=%fused_computation.13 | convolution fusion | flops 67174400 | bytes 1179648 | tf_op jit(solution)/shard_map/dot_general | solution.py:20
  39.1 1.3 %convolution_add_fusion.12 = f32[128,512]{1,0:T(8,128)S(1)} fusion(f32[128,512]{1,0:T(8,128)S(1)} %convolution_add_fusion.13, bf16[128,512]{1,0:T(8,128)(2,1)S(1)} %reshape.166, bf16[1,9,512,512]{3,2,1,0:T(8,128)(2,1)} %param.9), kind=kOutput, calls=%fused_computation.12 | convolution fusion | flops 67174400 | bytes 1179648 | tf_op jit(solution)/shard_map/dot_general | solution.py:20
  40.4 1.3 %convolution_add_fusion.11 = f32[128,512]{1,0:T(8,128)S(1)} fusion(f32[128,512]{1,0:T(8,128)S(1)} %convolution_add_fusion.12, bf16[128,512]{1,0:T(8,128)(2,1)S(1)} %reshape.172, bf16[1,9,512,512]{3,2,1,0:T(8,128)(2,1)} %param.9), kind=kOutput, calls=%fused_computation.11 | convolution fusion | flops 67174400 | bytes 1179648 | tf_op jit(solution)/shard_map/dot_general | solution.py:20
  41.7 1.3 %convolution_add_fusion.10 = f32[128,512]{1,0:T(8,128)S(1)} fusion(f32[128,512]{1,0:T(8,128)S(1)} %convolution_add_fusion.11, bf16[128,512]{1,0:T(8,128)(2,1)S(1)} %reshape.173, bf16[1,9,512,512]{3,2,1,0:T(8,128)(2,1)} %param.9), kind=kOutput, calls=%fused_computation.10 | convolution fusion | flops 67174400 | bytes 1179648 | tf_op jit(solution)/shard_map/dot_general | solution.py:20
  43.0 1.3 %convolution_add_fusion.9 = f32[128,512]{1,0:T(8,128)S(1)} fusion(f32[128,512]{1,0:T(8,128)S(1)} %convolution_add_fusion.10, bf16[128,512]{1,0:T(8,128)(2,1)S(1)} %reshape.174, bf16[1,9,512,512]{3,2,1,0:T(8,128)(2,1)} %param.9), kind=kOutput, calls=%fused_computation.9 | convolution fusion | flops 67174400 | bytes 1179648 | tf_op jit(solution)/shard_map/dot_general | solution.py:20
  44.3 1.3 %fusion.3 = bf16[128,512]{1,0:T(8,128)(2,1)S(1)} fusion(f32[128,512]{1,0:T(8,128)S(1)} %convolution_add_fusion.9, bf16[128,512]{1,0:T(8,128)(2,1)S(1)} %reshape.175, bf16[1,9,512,512]{3,2,1,0:T(8,128)(2,1)} %param.9), kind=kOutput, calls=%fused_computation.19 | convolution fusion | flops 67305472 | bytes 1048576 | tf_op jit(solution)/shard_map/dot_general | solution.py:20
  46.2 1.3 %fusion.12 = f32[128,512]{1,0:T(8,128)S(1)} fusion(bf16[128,512]{1,0:T(8,128)(2,1)S(1)} %reshape.177, bf16[1,9,512,512]{3,2,1,0:T(8,128)(2,1)} %param.10), kind=kOutput, calls=%fused_computation.44 | convolution fusion | flops 67108864 | bytes 917504 | tf_op jit(solution)/shard_map/dot_general | solution.py:20
  47.5 1.3 %convolution_add_fusion.7 = f32[128,512]{1,0:T(8,128)S(1)} fusion(f32[128,512]{1,0:T(8,128)S(1)} %fusion.12, bf16[128,512]{1,0:T(8,128)(2,1)S(1)} %reshape.178, bf16[1,9,512,512]{3,2,1,0:T(8,128)(2,1)} %param.10), kind=kOutput, calls=%fused_computation.7 | convolution fusion | flops 67174400 | bytes 1179648 | tf_op jit(solution)/shard_map/dot_general | solution.py:20
  48.8 1.3 %convolution_add_fusion.6 = f32[128,512]{1,0:T(8,128)S(1)} fusion(f32[128,512]{1,0:T(8,128)S(1)} %convolution_add_fusion.7, bf16[128,512]{1,0:T(8,128)(2,1)S(1)} %reshape.179, bf16[1,9,512,512]{3,2,1,0:T(8,128)(2,1)} %param.10), kind=kOutput, calls=%fused_computation.6 | convolution fusion | flops 67174400 | bytes 1179648 | tf_op jit(solution)/shard_map/dot_general | solution.py:20
  50.1 1.3 %convolution_add_fusion.5 = f32[128,512]{1,0:T(8,128)S(1)} fusion(f32[128,512]{1,0:T(8,128)S(1)} %convolution_add_fusion.6, bf16[128,512]{1,0:T(8,128)(2,1)S(1)} %reshape.180, bf16[1,9,512,512]{3,2,1,0:T(8,128)(2,1)} %param.10), kind=kOutput, calls=%fused_computation.5 | convolution fusion | flops 67174400 | bytes 1179648 | tf_op jit(solution)/shard_map/dot_general | solution.py:20
  51.4 1.3 %convolution_add_fusion.4 = f32[128,512]{1,0:T(8,128)S(1)} fusion(f32[128,512]{1,0:T(8,128)S(1)} %convolution_add_fusion.5, bf16[128,512]{1,0:T(8,128)(2,1)S(1)} %fusion.3, bf16[1,9,512,512]{3,2,1,0:T(8,128)(2,1)} %param.10), kind=kOutput, calls=%fused_computation.4 | convolution fusion | flops 67174400 | bytes 1179648 | tf_op jit(solution)/shard_map/dot_general | solution.py:20
  52.8 1.3 %convolution_add_fusion.3 = f32[128,512]{1,0:T(8,128)S(1)} fusion(f32[128,512]{1,0:T(8,128)S(1)} %convolution_add_fusion.4, bf16[128,512]{1,0:T(8,128)(2,1)S(1)} %reshape.181, bf16[1,9,512,512]{3,2,1,0:T(8,128)(2,1)} %param.10), kind=kOutput, calls=%fused_computation.3 | convolution fusion | flops 67174400 | bytes 1179648 | tf_op jit(solution)/shard_map/dot_general | solution.py:20
  54.1 1.3 %convolution_add_fusion.2 = f32[128,512]{1,0:T(8,128)S(1)} fusion(f32[128,512]{1,0:T(8,128)S(1)} %convolution_add_fusion.3, bf16[128,512]{1,0:T(8,128)(2,1)S(1)} %reshape.182, bf16[1,9,512,512]{3,2,1,0:T(8,128)(2,1)} %param.10), kind=kOutput, calls=%fused_computation.2 | convolution fusion | flops 67174400 | bytes 1179648 | tf_op jit(solution)/shard_map/dot_general | solution.py:20
  55.4 1.3 %convolution_add_fusion.1 = f32[128,512]{1,0:T(8,128)S(1)} fusion(f32[128,512]{1,0:T(8,128)S(1)} %convolution_add_fusion.2, bf16[128,512]{1,0:T(8,128)(2,1)S(1)} %reshape.183, bf16[1,9,512,512]{3,2,1,0:T(8,128)(2,1)} %param.10), kind=kOutput, calls=%fused_computation.1 | convolution fusion | flops 67174400 | bytes 1179648 | tf_op jit(solution)/shard_map/dot_general | solution.py:20
  56.7 1.3 %bitcast_reduce_fusion = f32[8,512]{1,0:T(8,128)S(1)} fusion(f32[128,512]{1,0:T(8,128)S(1)} %convolution_add_fusion.1, bf16[128,512]{1,0:T(8,128)(2,1)S(1)} %reshape.184, bf16[1,9,512,512]{3,2,1,0:T(8,128)(2,1)} %param.10, bf16[128,512]{1,0:T(8,128)(2,1)S(1)} %reshape.166), kind=kOutput, calls=%fused_computation.74 | convolution fusion | flops 67432448 | bytes 1064960 | tf_op jit(solution)/shard_map/dot_general | solution.py:20
  63.1 1.2 %constant_dynamic-update-slice_fusion.4 = f32[8,1,1]{2,1,0:T(1,128)} fusion(f32[8,1,1]{2,1,0:T(1,128)} %constant_dynamic-update-slice_fusion.5, f32[1,1,1]{2,1,0:T(1,128)} %bitcast.23), kind=kLoop, calls=%fused_computation.82 | loop fusion | bytes 1024
  65.4 1.2 %constant_dynamic-update-slice_fusion.2 = f32[8,1,1]{2,1,0:T(1,128)} fusion(f32[8,1,1]{2,1,0:T(1,128)} %constant_dynamic-update-slice_fusion.3, f32[1,1,1]{2,1,0:T(1,128)} %bitcast.25), kind=kLoop, calls=%fused_computation.80 | loop fusion | bytes 1024
  66.6 1.2 %constant_dynamic-update-slice_fusion.1 = f32[8,1,1]{2,1,0:T(1,128)} fusion(f32[8,1,1]{2,1,0:T(1,128)} %constant_dynamic-update-slice_fusion.2, f32[1,1,1]{2,1,0:T(1,128)} %bitcast.26), kind=kLoop, calls=%fused_computation.79 | loop fusion | bytes 1024
  70.3 5.5 %all-to-all-start = ((f32[8,1,1]{2,1,0:T(1,128)}), f32[8,1,1]{2,1,0:T(1,128)S(1)}, u32[]{:S(2)}, u32[]{:S(2)}) async-start(f32[8,1,1]{2,1,0:T(1,128)} %constant_dynamic-update-slice_fusion), calls=%async_computation | async-start | bytes 8192 | tf_op jit(solution)/shard_map/all_to_all | solution.py:66
  75.8 11.9 %all-reduce.2 = s32[8]{0:T(128)S(1)} all-reduce(s32[8]{0:T(128)S(1)} %dynamic-update-slice), channel_id=1, replica_groups=mesh['mp'=8,'dp'=4] {'mp'}, use_global_device_ids=true, to_apply=%add.2 | all-reduce | flops 8 | bytes 64
  (42 shorter events, 11.7 us)
Async XLA Ops:
  48.8 9.2 %copy-start = (f32[1,512,10]{1,0,2:T(1,128)S(1)}, f32[1,512,10]{1,0,2:T(1,128)}, u32[]{:S(2)}) copy-start(f32[1,512,10]{1,0,2:T(1,128)} %param.11) | copy-start | bytes 61444
  48.8 9.2 %copy-start.1 = (s32[8]{0:T(128)S(1)}, s32[8]{0:T(128)}, u32[]{:S(2)}) copy-start(s32[8]{0:T(128)} %param.7) | copy-start | bytes 100
  48.8 20.1 %copy-start.2 = (u32[32]{0:T(128)S(1)}, u32[32]{0:T(128)}, u32[]{:S(2)}) copy-start(u32[32]{0:T(128)} %constant.32) | copy-start | bytes 388
  70.3 17.4 %all-to-all-start = ((f32[8,1,1]{2,1,0:T(1,128)}), f32[8,1,1]{2,1,0:T(1,128)S(1)}, u32[]{:S(2)}, u32[]{:S(2)}) async-start(f32[8,1,1]{2,1,0:T(1,128)} %constant_dynamic-update-slice_fusion), calls=%async_computation | async-start | bytes 8192 | tf_op jit(solution)/shard_map/all_to_all | solution.py:66
